TPU v7x, 32 devices: a whole 2x2x4 slice. The times are simulated.
32 devices in a mesh: half: 2 (over core), blk: 4 (over z), sub: 4 (over y, x).
Axes of the slice: x: 2, y: 2, z: 4, core: 2. Of those that a mesh axis runs over, the one named last changes fastest.
Arguments:
- leaf_expansions: float32 [16384, 128], P(('half', 'blk', 'sub')), may hold values from -0.3 to 0.3
- leaf_occupied: int32 [16384], P(('half', 'blk', 'sub')), may hold values 0 or 1
- cone_angles: float32 [2, 48], replicated, may hold values from -3.140625 to 3.140625
- cone_need3: int32 [48, 32], P(('half', 'blk'), 'sub'), may hold values 0 or 1
- cone_need4: int32 [48, 4], P(('half', 'blk'), 'sub'), may hold values 0 or 1
Outputs:
- lowfreq: float32 [256, 128], P(('half', 'blk', 'sub'))
- cone_expansions: float32 [48, 4, 128], P(('half', 'blk'), 'sub')
All inputs are finite; a program needn't handle non-finite values. No bound on the sum of `leaf_occupied` or of `cone_need3` or of `cone_need4` on one device may be relied on, other than what follows from the above.
Results may differ from a plain program's by a relative error of at most 0.00007.
Values sent between devices are 32-bit elements; how exact they have to be, the bound alone decides.
A program may use at most 64 MiB of HBM per device.

v0:
```python
import math

import jax
import jax.numpy as jnp
from jax import lax
from jax.sharding import PartitionSpec as P

ORDER = 4


near_scale = 1.5
far_scale = 3.0
highest = lax.Precision.HIGHEST


def chebyshev_points(per_axis):
    index = jnp.arange(per_axis, dtype=jnp.float32)
    return jnp.cos((2.0 * index + 1.0) * math.pi / (2.0 * per_axis))


def octant_signs():
    octant = jnp.arange(8, dtype=jnp.int32)
    bits = jnp.stack([octant // 4 % 2, octant // 2 % 2, octant % 2], -1)
    return bits.astype(jnp.float32) * 2.0 - 1.0


def octant_table(per_axis):
    points = chebyshev_points(per_axis)
    degree = jnp.arange(1, per_axis, dtype=jnp.float32)
    sign_pair = jnp.array([-1.0, 1.0], dtype=jnp.float32)
    shifted = (points[None, :] + sign_pair[:, None]) / 2.0
    poly_here = jnp.cos(degree[None, :] * jnp.arccos(points)[:, None])
    poly_there = jnp.cos(degree[None, None, :] * jnp.arccos(shifted)[:, :, None])
    single = 1.0 / per_axis + 2.0 / per_axis * jnp.einsum(
        "mk,bnk->bmn", poly_here, poly_there, precision=highest
    )
    signs = octant_signs()
    along_x = jnp.where((signs[:, 0] > 0)[:, None, None], single[1][None], single[0][None])
    along_y = jnp.where((signs[:, 1] > 0)[:, None, None], single[1][None], single[0][None])
    along_z = jnp.where((signs[:, 2] > 0)[:, None, None], single[1][None], single[0][None])
    full = jnp.einsum("oad,obe,ocf->odefabc", along_x, along_y, along_z, precision=highest)
    node_count = per_axis**3
    return full.reshape(8, node_count, node_count)


def node_offsets(per_axis):
    points = chebyshev_points(per_axis)
    index = jnp.arange(per_axis**3, dtype=jnp.int32)
    coords = jnp.stack(
        [
            points[index // (per_axis * per_axis)],
            points[index // per_axis % per_axis],
            points[index % per_axis],
        ],
        -1,
    )
    return coords[None, :, :] + octant_signs()[:, None, :]


def phases(angles, strength, per_axis):
    polar = angles[0]
    azimuth = angles[1]
    direction = jnp.stack(
        [jnp.sin(polar) * jnp.cos(azimuth), jnp.sin(polar) * jnp.sin(azimuth), jnp.cos(polar)], -1
    )
    offsets = node_offsets(per_axis)
    argument = offsets[None, :, :, 0] * direction[:, None, None, 0]
    argument = argument + offsets[None, :, :, 1] * direction[:, None, None, 1]
    argument = argument + offsets[None, :, :, 2] * direction[:, None, None, 2]
    argument = -strength * argument
    return (jnp.cos(argument), jnp.sin(argument))


def block_count(length, target):
    number = 1
    while length % (2 * number) == 0 and length // (2 * number) >= target:
        number = number * 2
    return number


def cone_products(box_data, cosines, sine_part, transfer):
    real_part = box_data[:, :, 0, :]
    imag_part = box_data[:, :, 1, :]
    mod_real = cosines[:, None] * real_part[None] - sine_part[:, None] * imag_part[None]
    mod_imag = cosines[:, None] * imag_part[None] + sine_part[:, None] * real_part[None]
    out_real = jnp.einsum("cbon,onm->cbm", mod_real, transfer, precision=highest)
    out_imag = jnp.einsum("cbon,onm->cbm", mod_imag, transfer, precision=highest)
    return jnp.concatenate([out_real, out_imag], -1)


def local(leaf_expansions, leaf_occupied, cone_angles, cone_need3, cone_need4):
    width = leaf_expansions.shape[1]
    node_count = width // 2
    subs = lax.axis_size("sub")
    groups = lax.axis_size("half") * lax.axis_size("blk")
    cone_local = cone_need3.shape[0]
    transfer = octant_table(ORDER)
    masked = leaf_expansions * leaf_occupied.astype(jnp.float32)[:, None]
    level_one_count = masked.shape[0] // 8
    pair_count = level_one_count // 2
    per_sub = pair_count // subs
    per_box = per_sub // 8
    masked = masked.reshape(level_one_count, 8, 2, node_count)
    level_one = jnp.einsum("poan,onm->pam", masked, transfer, precision=highest)
    level_one = level_one.reshape(pair_count, 2, 2, node_count)
    moved = lax.all_to_all(level_one, "sub", split_axis=0, concat_axis=1, tiled=True)
    lowfreq = jnp.einsum("koan,onm->kam", moved, transfer, precision=highest).reshape(
        per_sub, width
    )
    own_angles = lax.dynamic_slice_in_dim(
        cone_angles, lax.axis_index(("half", "blk")) * cone_local, cone_local, 1
    )
    cos_near, sin_near = phases(cone_angles, near_scale, ORDER)
    cone_total = cos_near.shape[0]
    blocks = block_count(cone_total, 128)
    block_size = cone_total // blocks
    box_data = lowfreq.reshape(per_box, 8, 2, node_count)

    def one_block(inputs):
        return cone_products(box_data, inputs[0], inputs[1], transfer)

    stacked = lax.map(
        one_block,
        (
            cos_near.reshape(blocks, block_size, 8, node_count),
            sin_near.reshape(blocks, block_size, 8, node_count),
        ),
    )
    level_three = stacked.reshape(cone_total, per_box, width)
    received = lax.all_to_all(level_three, ("half", "blk"), split_axis=0, concat_axis=1, tiled=True)
    received = received * cone_need3.astype(jnp.float32)[:, :, None]
    received = received.reshape(cone_local, groups // 8, 8, per_box, 2, node_count)
    cos_far, sin_far = phases(own_angles, far_scale, ORDER)
    real_part = received[:, :, :, :, 0, :]
    imag_part = received[:, :, :, :, 1, :]
    cos_wide = cos_far[:, None, :, None, :]
    sin_wide = sin_far[:, None, :, None, :]
    mod_real = cos_wide * real_part - sin_wide * imag_part
    mod_imag = cos_wide * imag_part + sin_wide * real_part
    four_real = jnp.einsum("cqotn,onm->cqtm", mod_real, transfer, precision=highest)
    four_imag = jnp.einsum("cqotn,onm->cqtm", mod_imag, transfer, precision=highest)
    joined = jnp.concatenate([four_real, four_imag], -1).reshape(cone_local, -1, width)
    cone_expansions = joined * cone_need4.astype(jnp.float32)[:, :, None]
    return (lowfreq, cone_expansions)


def solution(mesh):
    return jax.shard_map(
        local,
        mesh=mesh,
        in_specs=(
            P(("half", "blk", "sub"), None),
            P(("half", "blk", "sub")),
            P(),
            P(("half", "blk"), "sub"),
            P(("half", "blk"), "sub"),
        ),
        out_specs=(P(("half", "blk", "sub"), None), P(("half", "blk"), "sub", None)),
        check_vma=False,
    )
```

profile of v0, /device:TPU:0, one launch (start us, length us, event | category | flops | bytes accessed | tf_op | source)
XLA Modules:
  0.0 33.9 jit_solution(4536432262568646164)
XLA Ops:
  0.9 0.8 %sqrt_atan2_fusion = f32[2,4]{1,0:T(2,128)S(1)} fusion(f32[2]{0:T(128)} %constant.187.clone, f32[4]{0:T(128)S(1)} %multiply_cosine_fusion), kind=kLoop, calls=%fused_computation.109 | loop fusion | flops 40 | bytes 56 | tf_op jit(solution)/shard_map/acos | solution.py:33
  1.6 0.3 fusion.1
  2.1 0.5 %broadcast_multiply_fusion = f32[8,4,4,4,4,4,4]{0,5,1,3,6,2,4:T(4,128)S(1)} fusion(f32[8,4,4]{0,1,2:T(4,128)S(1)} %get-tuple-element.39, f32[8,4,4,4,4]{0,1,3,2,4:T(4,128)S(1)} %broadcast_multiply_fusion.2), kind=kLoop, calls=%fused_computation.8 | loop fusion | flops 32768 | bytes 139776 | tf_op jit(solution)/shard_map/oad,obe,ocf->odefabc/dot_general | solution.py:41
  2.6 0.6 %copy.73 = f32[8,64,64,1,1]{2,1,0,4,3:T(8,128)S(1)} copy(f32[8,64,64,1,1]{0,2,1,4,3:T(8,128)S(1)} %bitcast.100) | data formatting | bytes 262144 | tf_op jit(solution)/shard_map/reshape | solution.py:43
  3.4 0.3 reshape.564
  3.7 0.8 %convolution_bitcast_fusion = f32[32,2,2,64]{3,0,2,1:T(8,128)S(1)} fusion(f32[8,64,64,1,1]{2,1,0,4,3:T(8,128)S(1)} %copy.73, f32[32,2,2,64,8]{3,2,4,1,0:T(2,128)S(1)} %bitcast.102), kind=kOutput, calls=%fused_computation | convolution fusion | flops 50331648 | bytes 425984 | tf_op jit(solution)/shard_map/poan,onm->pam/dot_general | solution.py:104
  4.6 0.7 %reshape.658 = f32[4,1,2048]{2,1,0:T(1,128)} reshape(f32[32,2,2,64]{3,2,1,0:T(2,128)S(1)} %copy.59) | data formatting | bytes 65536
  5.3 5.2 %all-to-all-start = ((f32[4,1,2048]{2,1,0:T(1,128)}), f32[4,1,2048]{2,1,0:T(1,128)S(1)}, u32[]{:S(2)}, u32[]{:S(2)}) async-start(f32[4,1,2048]{2,1,0:T(1,128)} %reshape.658), calls=%async_computation | async-start | bytes 65536 | tf_op jit(solution)/shard_map/all_to_all | solution.py:106
  10.5 0.6 %fusion.57 = (f32[1]{0:T(128)}, f32[1]{0:T(128)}, f32[1]{0:T(128)}, f32[1]{0:T(128)}) fusion(f32[4]{0:T(128)S(1)} %multiply_cosine_fusion), kind=kLoop, calls=%fused_computation.136 | loop fusion | bytes 32 | tf_op jit(solution)/shard_map/gather | solution.py:51
  11.1 2.5 %compare_select_fusion.9 = (f32[64,1]{0,1:T(1,128)S(1)}, f32[64,1]{0,1:T(1,128)S(1)}) fusion(f32[]{:T(128)} %bitcast.21, f32[]{:T(128)} %bitcast.22, f32[]{:T(128)} %bitcast.24, f32[]{:T(128)} %bitcast.23), kind=kLoop, calls=%fused_computation.83 | loop fusion | flops 2624 | bytes 528 | tf_op jit(solution)/shard_map/gather | solution.py:53
  13.6 2.5 %compare_select_fusion.15 = f32[64,1]{0,1:T(1,128)S(1)} fusion(f32[]{:T(128)} %bitcast.21, f32[]{:T(128)} %bitcast.22, f32[]{:T(128)} %bitcast.24, f32[]{:T(128)} %bitcast.23), kind=kLoop, calls=%fused_computation.89 | loop fusion | flops 1088 | bytes 272 | tf_op jit(solution)/shard_map/gather | solution.py:51
  16.4 0.6 %copy.61 = f32[8,64,64]{2,1,0:T(8,128)S(1)} copy(f32[8,64,64]{0,2,1:T(8,128)S(1)} %bitcast.101) | data formatting | bytes 262144 | tf_op jit(solution)/shard_map/reshape | solution.py:43
  17.0 0.5 %broadcast.791 = f32[]{:T(128)} broadcast(f32[]{:T(128)} %constant.300), dimensions={} | broadcast | bytes 8 | tf_op jit(solution)/shard_map/all_to_all | solution.py:106
  17.5 0.7 %reduce = f32[4,2048]{1,0:T(4,128)S(1)} reduce(f32[4,1,2048]{2,1,0:T(1,128)S(1)} %all-to-all-done, f32[]{:T(128)} %broadcast.791), dimensions={1}, to_apply=%all_to_all.26.reduce_sub_computation | reduce | bytes 65540 | tf_op jit(solution)/shard_map/all_to_all | solution.py:106
  18.4 0.3 fusion.3
  18.7 1.1 %convolution_bitcast_fusion.2 = f32[48,1,64]{2,0,1:T(8,128)S(1)} fusion(f32[8,64,64]{2,1,0:T(8,128)S(1)} %copy.61, f32[8,64]{1,0:T(8,128)S(1)} %get-tuple-element.36, f32[8,64]{1,0:T(8,128)S(1)} %get-tuple-element.35, f32[48]{0:T(128)S(1)} %get-tuple-element.50, f32[8,64]{1,0:T(8,128)S(1)} %get-tuple-element.33, f32[48]{0:T(128)S(1)} %get-tuple-element.49, ...), kind=kOutput, calls=%fused_computation.2 | convolution fusion | flops 19095552 | bytes 154176 | tf_op jit(solution)/shard_map/while/body/eval_jaxpr/cbon,onm->cbm/dot_general | solution.py:86
  19.8 1.1 %convolution_bitcast_fusion.1 = f32[48,1,64]{2,0,1:T(8,128)S(1)} fusion(f32[8,64,64]{2,1,0:T(8,128)S(1)} %copy.61, f32[8,64]{1,0:T(8,128)S(1)} %get-tuple-element.36, f32[8,64]{1,0:T(8,128)S(1)} %get-tuple-element.35, f32[48]{0:T(128)S(1)} %get-tuple-element.50, f32[8,64]{1,0:T(8,128)S(1)} %get-tuple-element.33, f32[48]{0:T(128)S(1)} %get-tuple-element.49, ...), kind=kOutput, calls=%fused_computation.1 | convolution fusion | flops 19095552 | bytes 154176 | tf_op jit(solution)/shard_map/while/body/eval_jaxpr/cbon,onm->cbm/dot_general | solution.py:87
  20.9 0.7 %pad_maximum_fusion = f32[48,1,128]{2,0,1:T(8,128)} fusion(f32[48,1,64]{2,0,1:T(8,128)S(1)} %convolution_bitcast_fusion.1, f32[48,1,64]{2,0,1:T(8,128)S(1)} %convolution_bitcast_fusion.2), kind=kLoop, calls=%fused_computation.43 | loop fusion | flops 6144 | bytes 49152 | tf_op jit(solution)/shard_map/while/body/eval_jaxpr/concatenate | solution.py:88
  21.6 4.9 %all-to-all-start.1 = ((f32[48,1,128]{2,1,0:T(1,128)}), f32[48,1,128]{2,1,0:T(1,128)S(1)}, u32[]{:S(2)}, u32[]{:S(2)}) async-start(f32[48,1,128]{2,1,0:T(1,128)} %bitcast.41), calls=%async_computation.1 | async-start | bytes 49152 | tf_op jit(solution)/shard_map/all_to_all | solution.py:130
  26.5 0.7 %reshape.566 = f32[8,128]{1,0:T(8,128)} reshape(f32[8,2,64]{2,1,0:T(2,128)S(1)} %copy.62) | data formatting | bytes 8192 | tf_op jit(solution)/shard_map/reshape | solution.py:107
  27.2 5.0 %all-to-all-done.1 = f32[48,1,128]{2,1,0:T(1,128)S(1)} async-done(((f32[48,1,128]{2,1,0:T(1,128)}), f32[48,1,128]{2,1,0:T(1,128)S(1)}, u32[]{:S(2)}, u32[]{:S(2)}) %all-to-all-start.1) | async-done | bytes 24608 | tf_op jit(solution)/shard_map/all_to_all | solution.py:130
  32.7 0.3 convolution_bitcast_fusion.4
  32.9 0.3 convolution_bitcast_fusion.3
  33.3 0.6 %copy.72 = f32[6,1,128]{2,1,0:T(1,128)} copy(f32[6,1,128]{2,0,1:T(8,128)S(1)} %fusion.39) | data formatting | bytes 6144
  (42 shorter events, 1.4 us)
Async XLA Ops:
  2.0 1.2 %copy-start.3 = (s32[512]{0:T(512)S(1)}, s32[512]{0:T(512)}, u32[]{:S(2)}) copy-start(s32[512]{0:T(512)} %param.7) | copy-start | bytes 6148
  2.0 1.2 %copy-start = (f32[512,128]{1,0:T(8,128)S(1)}, f32[512,128]{1,0:T(8,128)}, u32[]{:S(2)}) copy-start(f32[512,128]{1,0:T(8,128)} %param.6) | copy-start | bytes 786436
  2.6 13.6 %copy-start.2 = (f32[2,48]{1,0:T(2,128)S(1)}, f32[2,48]{1,0:T(2,128)}, u32[]{:S(2)}) copy-start(f32[2,48]{1,0:T(2,128)} %param.8) | copy-start | bytes 1156
  5.3 11.7 %all-to-all-start = ((f32[4,1,2048]{2,1,0:T(1,128)}), f32[4,1,2048]{2,1,0:T(1,128)S(1)}, u32[]{:S(2)}, u32[]{:S(2)}) async-start(f32[4,1,2048]{2,1,0:T(1,128)} %reshape.658), calls=%async_computation | async-start | bytes 65536 | tf_op jit(solution)/shard_map/all_to_all | solution.py:106
  16.4 10.1 %copy-start.4 = (s32[6,1]{0,1:T(1,128)S(1)}, s32[6,1]{0,1:T(1,128)}, u32[]{:S(2)}) copy-start(s32[6,1]{0,1:T(1,128)} %param.10) | copy-start | bytes 76
  16.4 10.1 %copy-start.1 = (s32[6,8]{1,0:T(8,128)S(1)}, s32[6,8]{1,0:T(8,128)}, u32[]{:S(2)}) copy-start(s32[6,8]{1,0:T(8,128)} %param.9) | copy-start | bytes 580
  21.6 10.6 %all-to-all-start.1 = ((f32[48,1,128]{2,1,0:T(1,128)}), f32[48,1,128]{2,1,0:T(1,128)S(1)}, u32[]{:S(2)}, u32[]{:S(2)}) async-start(f32[48,1,128]{2,1,0:T(1,128)} %bitcast.41), calls=%async_computation.1 | async-start | bytes 49152 | tf_op jit(solution)/shard_map/all_to_all | solution.py:130
where the time goes:
time: 34.2 us; the launch traced here: 33.9 us
  starting transfers between devices  10.1 us (30%)
  other arithmetic  8.68 us (25%)
  local copies, waits for them, and re-layouts  5.09 us (15%)
  waiting for transfers between devices  5.01 us (15%)
  matrix products  4.13 us (12%)
  between operations  0.92 us (3%)
    all_to_all x1, starting transfers between devices, local(): lax.all_to_all(level_one, 'sub', split_axis=0, concat_axis=1, tiled=True)  5.19 us
    all_to_all x1, waiting for transfers between devices, local(): lax.all_to_all(level_three, ('half', 'blk'), split_axis=0, concat_axis=1,...  5.01 us
    all_to_all x1, starting transfers between devices, local(): lax.all_to_all(level_three, ('half', 'blk'), split_axis=0, concat_axis=1,...  4.88 us
    gather x1, other arithmetic, node_offsets(): points[index % per_axis]  2.49 us
    gather x1, other arithmetic, node_offsets(): points[index // (per_axis * per_axis)]  2.49 us
    unnamed x13, local copies, waits for them, and re-layouts  1.46 us
    reshape x2, local copies, waits for them, and re-layouts, octant_table(): return full.reshape(8, node_count, node_count)  1.24 us
    dot_general x1, matrix products, cone_products(): jnp.einsum('cbon,onm->cbm', mod_real, transfer, precision=highest)  1.11 us
  transfers between devices with their start and end apart: 2, of which 1 were waited for; matrix products, arithmetic and copies ran while one was open for 21% of the time, Pallas kernels for 0%

commit v1 on v0

v1 whole, which is shorter than its diff:
```python
import functools
import math

import jax
import jax.numpy as jnp
import numpy as np
from jax import lax
from jax.experimental import pallas as pl
from jax.experimental.pallas import tpu as pltpu
from jax.sharding import PartitionSpec as P

MESH = pl.DeviceIdType.MESH
F32, BF16 = jnp.float32, jnp.bfloat16
ORDER = 4
OCT = 8
NEAR = 1.5


def octant_signs():
    octant = np.arange(OCT)
    return np.stack([octant // 4 % 2, octant // 2 % 2, octant % 2], -1) * 2.0 - 1.0


def chebyshev_points(per_axis):
    return np.cos((2.0 * np.arange(per_axis) + 1.0) * math.pi / (2.0 * per_axis))


def octant_table(per_axis):
    points = chebyshev_points(per_axis)
    degree = np.arange(1, per_axis)
    shifted = (points[None, :] + np.array([-1.0, 1.0])[:, None]) / 2.0
    here = np.cos(degree[None, :] * np.arccos(points)[:, None])
    there = np.cos(degree * np.arccos(shifted)[:, :, None])
    single = 1.0 / per_axis + 2.0 / per_axis * np.einsum("mk,bnk->bnm", here, there)
    bit = (octant_signs() > 0).astype(int)
    full = np.einsum("oda,oeb,ofc->odefabc", single[bit[:, 0]], single[bit[:, 1]], single[bit[:, 2]])
    return full.reshape(OCT, per_axis**3, per_axis**3)


def weight_table(per_axis):
    table = octant_table(per_axis).astype(np.float32)
    nodes = per_axis**3
    wide = np.zeros((OCT, 2, nodes, 2, nodes), np.float32)
    wide[:, 0, :, 0, :] = table
    wide[:, 1, :, 1, :] = table
    wide = wide.reshape(OCT * 2 * nodes, 2 * nodes)
    high = wide.astype(BF16)
    low = (wide - high.astype(np.float32)).astype(BF16)
    return np.concatenate([high, low], 1)


def lane_table(per_axis):
    points = chebyshev_points(per_axis)
    index = np.arange(per_axis**3)
    coords = np.stack([points[index // per_axis**2], points[index // per_axis % per_axis], points[index % per_axis]])
    offsets = coords[:, None, :] + octant_signs().T[:, :, None]
    offsets = -NEAR * np.concatenate([offsets, offsets], -1).reshape(3, -1)
    sign = np.tile(np.repeat([-1.0, 1.0], per_axis**3), OCT)
    return np.concatenate([offsets, sign[None]], 0).astype(np.float32)


def each(count, body):
    if count <= 16:
        for d in range(1, count):
            body(d)
    else:
        lax.fori_loop(1, count, lambda d, c: (body(d), c)[1], 0)


def split_rows(value):
    high = value.astype(BF16)
    low = (value - high.astype(F32)).astype(BF16)
    return jnp.concatenate([high, low], 0)


def fold(acc, rows, width):
    return (acc[:rows, :width] + acc[rows:, :width]) + (acc[:rows, width:] + acc[rows:, width:])


def kernel(
    halves, blks, subs, cones,
    leaf_hbm, occ_hbm, angle_hbm, need3_hbm, need4_hbm, weight_hbm, lane_hbm,
    low_out, cone_out,
    leaf, occ, angle, need3, need4, weight, lane, part, got, low, phase,
    in_sem, send1, recv1, send2, recv2,
):
    groups = halves * blks
    half, blk, sub = lax.axis_index("half"), lax.axis_index("blk"), lax.axis_index("sub")
    group = half * blks + blk
    rows, width = leaf.shape
    pairs = rows // (2 * OCT)
    per_sub = pairs // subs

    loads = [
        pltpu.make_async_copy(src, dst, in_sem.at[i])
        for i, (src, dst) in enumerate([
            (occ_hbm, occ), (leaf_hbm, leaf), (weight_hbm, weight), (angle_hbm, angle),
            (lane_hbm, lane), (need3_hbm, need3), (need4_hbm, need4),
        ])
    ]
    for load in loads:
        load.start()

    def sub_peer(d):
        return {"sub": lax.rem(sub + d, subs)}

    def group_peer(d):
        peer = lax.rem(group + d, groups)
        return {"half": peer // blks, "blk": lax.rem(peer, blks)}

    barrier = pltpu.get_barrier_semaphore()

    def greet(peer, d):
        pl.semaphore_signal(barrier, inc=1, device_id=peer(d), device_id_type=MESH)

    each(groups, functools.partial(greet, group_peer))
    each(subs, functools.partial(greet, sub_peer))

    loads[0].wait()
    loads[1].wait()
    columns = jnp.transpose(occ[...].astype(F32))
    for i in range(rows // 128):
        chunk = pl.ds(i * 128, 128)
        leaf[chunk, :] = leaf[chunk, :] * columns[:, i : i + 1]
    loads[2].wait()
    acc = None
    for t in range(OCT // 2):
        tile = jnp.concatenate(
            [
                jnp.concatenate(
                    [leaf[pl.ds(OCT * r + o, pairs, stride=2 * OCT), :] for o in (2 * t, 2 * t + 1)], 1
                )
                for r in range(2)
            ],
            0,
        )
        term = jnp.dot(
            split_rows(tile), weight[2 * width * t : 2 * width * (t + 1), :], preferred_element_type=F32
        )
        acc = term if acc is None else acc + term
    one = fold(acc, 2 * pairs, width)
    tile = jnp.concatenate([one[:pairs], one[pairs:]], 1)
    mine = weight[pl.ds(pl.multiple_of(sub * 2 * width, 2 * width), 2 * width), :]
    part[...] = fold(jnp.dot(split_rows(tile), mine, preferred_element_type=F32), pairs, width)

    pl.semaphore_wait(barrier, (groups - 1) + (subs - 1))

    def rows_of(index):
        return pl.ds(pl.multiple_of(index * per_sub, 8), per_sub)

    def copy_one(d):
        return pltpu.make_async_remote_copy(
            src_ref=part.at[rows_of(lax.rem(sub + d, subs))],
            dst_ref=got.at[d],
            send_sem=send1.at[d],
            recv_sem=recv1.at[d],
            device_id=sub_peer(d),
            device_id_type=MESH,
        )

    each(subs, lambda d: copy_one(d).start())

    loads[3].wait()
    loads[4].wait()
    padded = phase.shape[1]
    count = angle.shape[1]
    pick = lax.broadcasted_iota(jnp.int32, (padded, count), 1) == (
        lax.broadcasted_iota(jnp.int32, (padded, count), 0) + group * cones
    )
    polar = jnp.sum(jnp.where(pick, angle[0:1, :], 0.0), 1, keepdims=True)
    azimuth = jnp.sum(jnp.where(pick, angle[1:2, :], 0.0), 1, keepdims=True)
    sin_polar = jnp.sin(polar)
    argument = (
        (sin_polar * jnp.cos(azimuth)) * lane[0:1, :]
        + (sin_polar * jnp.sin(azimuth)) * lane[1:2, :]
        + jnp.cos(polar) * lane[2:3, :]
    )
    cosine, sine = jnp.cos(argument), jnp.sin(argument)
    sign = lane[3:4, :]
    phase[0] = cosine
    phase[1] = sine * sign
    phase[2] = 1.0 - 2.0 * sine * sine
    phase[3] = 2.0 * sine * cosine * sign
    loads[5].wait()
    loads[6].wait()

    each(subs, lambda d: copy_one(d).wait())
    total = part[rows_of(sub), :]
    for d in range(1, subs):
        total = total + got[d]
    low[group] = total
    low_out[...] = total

    def copy_two(d):
        return pltpu.make_async_remote_copy(
            src_ref=low.at[group],
            dst_ref=low.at[group],
            send_sem=send2.at[d],
            recv_sem=recv2.at[d],
            device_id=group_peer(d),
            device_id_type=MESH,
        )

    each(groups, lambda d: copy_two(d).start())
    each(groups, lambda d: copy_two(d).wait())

    def widen(value):
        fill = padded - cones
        if fill:
            value = jnp.concatenate([value, jnp.zeros((fill, value.shape[1]), value.dtype)], 0)
        return value.astype(F32)

    keep3 = widen(need3[...])
    lanes4 = need4.shape[1]
    diagonal = lax.broadcasted_iota(jnp.int32, (padded, lanes4), 0) == lax.broadcasted_iota(
        jnp.int32, (padded, lanes4), 1
    )

    def product(pieces):
        rows_in = pieces[0].shape[0]
        acc = None
        for t in range(OCT // 2):
            tile = split_rows(jnp.concatenate(pieces[2 * t : 2 * t + 2], 1))
            term = jnp.dot(tile, weight[2 * width * t : 2 * width * (t + 1), :], preferred_element_type=F32)
            acc = term if acc is None else acc + term
        return fold(acc, rows_in, width)

    for q in range(groups // OCT):
        boxes = [low[q * OCT + g] for g in range(OCT)]
        turned = [pltpu.roll(box, width // 2, 1) for box in boxes]
        pieces = []
        for o in range(OCT):
            lanes = slice(o * width, (o + 1) * width)
            cos_o, sin_o = phase[0, :, lanes], phase[1, :, lanes]
            pieces.append(
                jnp.concatenate(
                    [cos_o * boxes[g][o : o + 1, :] + sin_o * turned[g][o : o + 1, :] for g in range(OCT)], 0
                )
            )
        three = product(pieces)
        pieces = []
        for o in range(OCT):
            lanes = slice(o * width, (o + 1) * width)
            column = q * OCT + o
            box = three[o * padded : (o + 1) * padded] * keep3[:, column : column + 1]
            pieces.append(phase[2, :, lanes] * box + phase[3, :, lanes] * pltpu.roll(box, width // 2, 1))
        keep4 = jnp.sum(jnp.where(diagonal, need4[q : q + 1, :].astype(F32), 0.0), 1, keepdims=True)
        four = product(pieces) * keep4
        cone_out[:, q, :] = four[:cones]


def solution(mesh):
    halves, blks, subs = mesh.shape["half"], mesh.shape["blk"], mesh.shape["sub"]
    groups = halves * blks

    def local(leaf, occupied, angles, need3, need4):
        rows, width = leaf.shape
        pairs = rows // (2 * OCT)
        per_sub = pairs // subs
        cones = need3.shape[0]
        padded = -(-cones // 8) * 8
        assert per_sub == OCT and need3.shape[1] == groups
        weight = jnp.asarray(weight_table(ORDER))
        lane = jnp.asarray(lane_table(ORDER))
        occupied = occupied.reshape(rows // 128, 128)
        need4 = need4.T
        vmem = pl.BlockSpec(memory_space=pltpu.VMEM)
        anywhere = pl.BlockSpec(memory_space=pl.ANY)
        return pl.pallas_call(
            functools.partial(kernel, halves, blks, subs, cones),
            out_shape=(
                jax.ShapeDtypeStruct((per_sub, width), F32),
                jax.ShapeDtypeStruct((cones, groups // OCT, width), F32),
            ),
            in_specs=[anywhere] * 7,
            out_specs=(vmem, vmem),
            scratch_shapes=[
                pltpu.VMEM(leaf.shape, F32),
                pltpu.VMEM(occupied.shape, jnp.int32),
                pltpu.VMEM(angles.shape, F32),
                pltpu.VMEM(need3.shape, jnp.int32),
                pltpu.VMEM(need4.shape, jnp.int32),
                pltpu.VMEM(weight.shape, BF16),
                pltpu.VMEM(lane.shape, F32),
                pltpu.VMEM((pairs, width), F32),
                pltpu.VMEM((subs, per_sub, width), F32),
                pltpu.VMEM((groups, per_sub, width), F32),
                pltpu.VMEM((4, padded, OCT * width), F32),
                pltpu.SemaphoreType.DMA((7,)),
                pltpu.SemaphoreType.DMA((subs,)),
                pltpu.SemaphoreType.DMA((subs,)),
                pltpu.SemaphoreType.DMA((groups,)),
                pltpu.SemaphoreType.DMA((groups,)),
            ],
            compiler_params=pltpu.CompilerParams(collective_id=0, has_side_effects=True),
            name="upward",
        )(leaf, occupied, angles, need3, need4, weight, lane)

    return jax.shard_map(
        local,
        mesh=mesh,
        in_specs=(
            P(("half", "blk", "sub"), None),
            P(("half", "blk", "sub")),
            P(),
            P(("half", "blk"), "sub"),
            P(("half", "blk"), "sub"),
        ),
        out_specs=(P(("half", "blk", "sub"), None), P(("half", "blk"), "sub", None)),
        check_vma=False,
    )
```

time: 34.2 us -> 16.6 us (0.49)
  Pallas kernels: 0 us -> 13.9 us
  starting transfers between devices: 10.1 us -> 0 us
  other arithmetic: 8.68 us -> 0 us
  waiting for transfers between devices: 5.01 us -> 0 us
  matrix products: 4.13 us -> 0 us
  local copies, waits for them, and re-layouts: 5.09 us -> 1.85 us
    pallas_call x0 -> x1, Pallas kernels: none -> 13.9 us  [local(): pl.pallas_call(functools.partial(kernel, halves, blks, subs, cones), out_...]
    all_to_all x2 -> x0, starting transfers between devices: 10.1 us -> none  [the longest x1 5.19 us: local(): lax.all_to_all(level_one, 'sub', split_axis=0, concat_axis=1, tiled=True)]
    all_to_all x2 -> x0, waiting for transfers between devices: 5.01 us -> none  [the longest x1 5.01 us: local(): lax.all_to_all(level_three, ('half', 'blk'), split_axis=0, concat_axis=1,...]
    gather x2 -> x0, other arithmetic: 4.98 us -> none  [the longest x1 2.49 us: node_offsets(): points[index % per_axis]]
    dot_general x7 -> x0, matrix products: 4.13 us -> none  [the longest x1 1.11 us: cone_products(): jnp.einsum('cbon,onm->cbm', mod_real, transfer, precision=highest)]
    reshape x4 -> x0, local copies, waits for them, and re-layouts: 2.23 us -> none  [the longest x2 1.24 us: octant_table(): return full.reshape(8, node_count, node_count)]
    another operation x3 -> x0, other arithmetic: 0.86 us -> none  [the longest x1 0.77 us: octant_table(): jnp.arccos(shifted)[:, :, None]]
    all_to_all x1 -> x0, other arithmetic: 0.73 us -> none  [local(): lax.all_to_all(level_one, 'sub', split_axis=0, concat_axis=1, tiled=True)]
  transfers between devices with their start and end apart: 2 -> 0, of which waited for: 1 -> 0; matrix products, arithmetic and copies ran while one was open for 21% -> 0% of each run, Pallas kernels for 0% -> 0%
where the time goes in v1:
time: 16.6 us; the launch traced here: 16.4 us
  Pallas kernels  13.9 us (84%)
  local copies, waits for them, and re-layouts  1.85 us (11%)
  between operations  0.65 us (4%)
    pallas_call x1, Pallas kernels, local(): pl.pallas_call(functools.partial(kernel, halves, blks, subs, cones), out_...  13.9 us
    unnamed x4, local copies, waits for them, and re-layouts  1.85 us

profile of v1, /device:TPU:0, one launch (start us, length us, event | category | flops | bytes accessed | tf_op | source)
XLA Modules:
  0.0 16.4 jit_solution(7059619872958984141)
XLA Ops:
  0.6 13.9 %upward.1 = (f32[8,128]{1,0:T(8,128)}, f32[6,1,128]{2,1,0:T(1,128)}) custom-call(f32[512,128]{1,0:T(8,128)} %leaf_hbm.1, s32[4,128]{1,0:T(4,128)} %bitcast.2, f32[2,48]{1,0:T(2,128)} %angle_hbm.1, s32[6,8]{1,0:T(8,128)} %need3_hbm.1, s32[1,6]{1,0:T(1,128)} %bitcast.3, bf16[1024,256]{1,0:T(8,128)(2,1)} %constant.4.clone.weight_hbm, ...), custom_call_target="tpu_custom_call" | custom-call | tf_op jit(solution)/shard_map/upward/pallas_call | solution.py:269
  14.6 0.0 copy-start
  14.6 1.3 %copy.11 = f32[8,128]{1,0:T(8,128)} copy(f32[8,128]{1,0:T(8,128)} %get-tuple-element.4) | data formatting | bytes 8192
  15.9 0.0 copy-done
  15.9 0.6 %copy.12 = f32[6,1,128]{2,1,0:T(1,128)} copy(f32[6,1,128]{2,1,0:T(1,128)S(1)} %copy-done) | data formatting | bytes 6144
Async XLA Ops:
  14.6 1.3 %copy-start = (f32[6,1,128]{2,1,0:T(1,128)S(1)}, f32[6,1,128]{2,1,0:T(1,128)}, u32[]{:S(2)}) copy-start(f32[6,1,128]{2,1,0:T(1,128)} %get-tuple-element.5) | copy-start | bytes 9220

commit v2 on v1

--- a/solution.py
+++ b/solution.py
@@ -60,7 +60,7 @@
 
 
 def each(count, body):
-    if count <= 16:
+    if count <= 64:
         for d in range(1, count):
             body(d)
     else:
@@ -82,7 +82,7 @@
     leaf_hbm, occ_hbm, angle_hbm, need3_hbm, need4_hbm, weight_hbm, lane_hbm,
     low_out, cone_out,
     leaf, occ, angle, need3, need4, weight, lane, part, got, low, phase,
-    in_sem, send1, recv1, send2, recv2,
+    in_sem, send, recv, send2, recv2,
 ):
     groups = halves * blks
     half, blk, sub = lax.axis_index("half"), lax.axis_index("blk"), lax.axis_index("sub")
@@ -101,20 +101,20 @@
     for load in loads:
         load.start()
 
-    def sub_peer(d):
-        return {"sub": lax.rem(sub + d, subs)}
-
-    def group_peer(d):
-        peer = lax.rem(group + d, groups)
-        return {"half": peer // blks, "blk": lax.rem(peer, blks)}
+    def peer(d):
+        there = lax.rem(blk + d // subs, blks)
+        return {"blk": there, "sub": lax.rem(sub + lax.rem(d, subs), subs)}
+
+    def half_peer(e):
+        return {"half": lax.rem(half + e, halves)}
 
     barrier = pltpu.get_barrier_semaphore()
 
-    def greet(peer, d):
-        pl.semaphore_signal(barrier, inc=1, device_id=peer(d), device_id_type=MESH)
-
-    each(groups, functools.partial(greet, group_peer))
-    each(subs, functools.partial(greet, sub_peer))
+    def greet(target):
+        pl.semaphore_signal(barrier, inc=1, device_id=target, device_id_type=MESH)
+
+    each(halves, lambda e: greet(half_peer(e)))
+    each(blks * subs, lambda d: greet(peer(d)))
 
     loads[0].wait()
     loads[1].wait()
@@ -143,22 +143,23 @@
     mine = weight[pl.ds(pl.multiple_of(sub * 2 * width, 2 * width), 2 * width), :]
     part[...] = fold(jnp.dot(split_rows(tile), mine, preferred_element_type=F32), pairs, width)
 
-    pl.semaphore_wait(barrier, (groups - 1) + (subs - 1))
+    pl.semaphore_wait(barrier, blks * subs + halves - 2)
 
     def rows_of(index):
         return pl.ds(pl.multiple_of(index * per_sub, 8), per_sub)
 
-    def copy_one(d):
+    def copy(d):
         return pltpu.make_async_remote_copy(
-            src_ref=part.at[rows_of(lax.rem(sub + d, subs))],
-            dst_ref=got.at[d],
-            send_sem=send1.at[d],
-            recv_sem=recv1.at[d],
-            device_id=sub_peer(d),
+            src_ref=part.at[rows_of(lax.rem(sub + lax.rem(d, subs), subs))],
+            dst_ref=got.at[blk, sub],
+            send_sem=send.at[d],
+            recv_sem=recv.at[d],
+            device_id=peer(d),
             device_id_type=MESH,
         )
 
-    each(subs, lambda d: copy_one(d).start())
+    each(blks * subs, lambda d: copy(d).start())
+    got[blk, sub] = part[rows_of(sub), :]
 
     loads[3].wait()
     loads[4].wait()
@@ -184,25 +185,30 @@
     loads[5].wait()
     loads[6].wait()
 
-    each(subs, lambda d: copy_one(d).wait())
-    total = part[rows_of(sub), :]
-    for d in range(1, subs):
-        total = total + got[d]
-    low[group] = total
-    low_out[...] = total
-
-    def copy_two(d):
+    def forward(index, e):
+        there = half * blks + index
         return pltpu.make_async_remote_copy(
-            src_ref=low.at[group],
-            dst_ref=low.at[group],
-            send_sem=send2.at[d],
-            recv_sem=recv2.at[d],
-            device_id=group_peer(d),
+            src_ref=low.at[there],
+            dst_ref=low.at[there],
+            send_sem=send2.at[index, e],
+            recv_sem=recv2.at[index, e],
+            device_id=half_peer(e),
             device_id_type=MESH,
         )
 
-    each(groups, lambda d: copy_two(d).start())
-    each(groups, lambda d: copy_two(d).wait())
+    for step in range(blks):
+        for t in range(subs):
+            d = step * subs + t
+            if d:
+                copy(d).wait()
+        there = lax.rem(blk + (blks - step) % blks, blks)
+        total = functools.reduce(jnp.add, [got[there, t] for t in range(subs)])
+        low[half * blks + there] = total
+        if step == 0:
+            low_out[...] = total
+        each(halves, lambda e: forward(there, e).start())
+    for step in range(blks):
+        each(halves, lambda e: forward(lax.rem(blk + step, blks), e).wait())
 
     def widen(value):
         fill = padded - cones
@@ -249,6 +255,17 @@
         cone_out[:, q, :] = four[:cones]
 
 
+def put_out(low_ref, cone_ref, low_out, cone_out, sems):
+    copies = [
+        pltpu.make_async_copy(low_ref, low_out, sems.at[0]),
+        pltpu.make_async_copy(cone_ref, cone_out, sems.at[1]),
+    ]
+    for copy in copies:
+        copy.start()
+    for copy in copies:
+        copy.wait()
+
+
 def solution(mesh):
     halves, blks, subs = mesh.shape["half"], mesh.shape["blk"], mesh.shape["sub"]
     groups = halves * blks
@@ -266,11 +283,11 @@
         need4 = need4.T
         vmem = pl.BlockSpec(memory_space=pltpu.VMEM)
         anywhere = pl.BlockSpec(memory_space=pl.ANY)
-        return pl.pallas_call(
+        results = pl.pallas_call(
             functools.partial(kernel, halves, blks, subs, cones),
             out_shape=(
-                jax.ShapeDtypeStruct((per_sub, width), F32),
-                jax.ShapeDtypeStruct((cones, groups // OCT, width), F32),
+                pltpu.VMEM((per_sub, width), F32),
+                pltpu.VMEM((cones, groups // OCT, width), F32),
             ),
             in_specs=[anywhere] * 7,
             out_specs=(vmem, vmem),
@@ -283,18 +300,27 @@
                 pltpu.VMEM(weight.shape, BF16),
                 pltpu.VMEM(lane.shape, F32),
                 pltpu.VMEM((pairs, width), F32),
-                pltpu.VMEM((subs, per_sub, width), F32),
+                pltpu.VMEM((blks, subs, per_sub, width), F32),
                 pltpu.VMEM((groups, per_sub, width), F32),
                 pltpu.VMEM((4, padded, OCT * width), F32),
                 pltpu.SemaphoreType.DMA((7,)),
-                pltpu.SemaphoreType.DMA((subs,)),
-                pltpu.SemaphoreType.DMA((subs,)),
-                pltpu.SemaphoreType.DMA((groups,)),
-                pltpu.SemaphoreType.DMA((groups,)),
+                pltpu.SemaphoreType.DMA((blks * subs,)),
+                pltpu.SemaphoreType.DMA((blks * subs,)),
+                pltpu.SemaphoreType.DMA((blks, halves)),
+                pltpu.SemaphoreType.DMA((blks, halves)),
             ],
             compiler_params=pltpu.CompilerParams(collective_id=0, has_side_effects=True),
             name="upward",
         )(leaf, occupied, angles, need3, need4, weight, lane)
+        results = [pltpu.with_memory_space_constraint(value, pltpu.VMEM) for value in results]
+        return pl.pallas_call(
+            put_out,
+            out_shape=[jax.ShapeDtypeStruct(value.shape, F32) for value in results],
+            in_specs=[vmem] * 2,
+            out_specs=[pl.BlockSpec(memory_space=pltpu.HBM)] * 2,
+            scratch_shapes=[pltpu.SemaphoreType.DMA((2,))],
+            name="put_out",
+        )(*results)
 
     return jax.shard_map(
         local,

time: 16.6 us -> 13.6 us (0.82)
  local copies, waits for them, and re-layouts: 1.85 us -> 0 us
  Pallas kernels: 13.9 us -> 12.8 us
    unnamed x4 -> x0, local copies, waits for them, and re-layouts: 1.85 us -> none
    pallas_call x1, Pallas kernels: 13.9 us -> 12.2 us  [local(): pl.pallas_call(functools.partial(kernel, halves, blks, subs, cones), out_...]
    pallas_call x0 -> x1, Pallas kernels: none -> 0.61 us  [local(): pl.pallas_call(put_out, out_shape=[jax.ShapeDtypeStruct(value.shape, F32)...]
where the time goes in v2:
time: 13.6 us; the launch traced here: 13.5 us
  Pallas kernels  12.8 us (94%)
  between operations  0.64 us (5%)
    pallas_call x1, Pallas kernels, local(): pl.pallas_call(functools.partial(kernel, halves, blks, subs, cones), out_...  12.2 us
    pallas_call x1, Pallas kernels, local(): pl.pallas_call(put_out, out_shape=[jax.ShapeDtypeStruct(value.shape, F32)...  0.61 us

profile of v2, /device:TPU:0, one launch (start us, length us, event | category | flops | bytes accessed | tf_op | source)
XLA Modules:
  0.0 13.5 jit_solution(1669062362527509252)
XLA Ops:
  0.6 12.2 %upward.1 = (f32[8,128]{1,0:T(8,128)S(1)}, f32[6,1,128]{2,1,0:T(1,128)S(1)}) custom-call(f32[512,128]{1,0:T(8,128)} %leaf_hbm.1, s32[4,128]{1,0:T(4,128)} %bitcast.2, f32[2,48]{1,0:T(2,128)} %angle_hbm.1, s32[6,8]{1,0:T(8,128)} %need3_hbm.1, s32[1,6]{1,0:T(1,128)} %bitcast.3, bf16[1024,256]{1,0:T(8,128)(2,1)} %constant.4.clone.weight_hbm, ...), custom_call_target="tpu_custom_call" | custom-call | tf_op jit(solution)/shard_map/upward/pallas_call | solution.py:286
  12.8 0.6 %put_out.1 = (f32[8,128]{1,0:T(8,128)}, f32[6,1,128]{2,1,0:T(1,128)}) custom-call(f32[8,128]{1,0:T(8,128)S(1)} %get-tuple-element.4.low_ref, f32[6,1,128]{2,1,0:T(1,128)S(1)} %get-tuple-element.5.cone_ref), custom_call_target="tpu_custom_call" | custom-call | tf_op jit(solution)/shard_map/put_out/pallas_call | solution.py:316

commit v3 on v2

--- a/solution.py
+++ b/solution.py
@@ -81,7 +81,7 @@
     halves, blks, subs, cones,
     leaf_hbm, occ_hbm, angle_hbm, need3_hbm, need4_hbm, weight_hbm, lane_hbm,
     low_out, cone_out,
-    leaf, occ, angle, need3, need4, weight, lane, part, got, low, phase,
+    leaf, occ, angle, need3, need4, weight, lane, part, got, low, three, phase,
     in_sem, send, recv, send2, recv2,
 ):
     groups = halves * blks
@@ -200,16 +200,13 @@
         for t in range(subs):
             d = step * subs + t
             if d:
-                copy(d).wait()
+                copy(d).wait_recv()
         there = lax.rem(blk + (blks - step) % blks, blks)
         total = functools.reduce(jnp.add, [got[there, t] for t in range(subs)])
         low[half * blks + there] = total
         if step == 0:
             low_out[...] = total
         each(halves, lambda e: forward(there, e).start())
-    for step in range(blks):
-        each(halves, lambda e: forward(lax.rem(blk + step, blks), e).wait())
-
     def widen(value):
         fill = padded - cones
         if fill:
@@ -231,28 +228,44 @@
             acc = term if acc is None else acc + term
         return fold(acc, rows_in, width)
 
+    def level_three(first):
+        size = min(blks, OCT)
+        for start in range(0, blks, size):
+            boxes = [low[first + start + g] for g in range(size)]
+            turned = [pltpu.roll(box, width // 2, 1) for box in boxes]
+            pieces = []
+            for o in range(OCT):
+                lanes = slice(o * width, (o + 1) * width)
+                cos_o, sin_o = phase[0, :, lanes], phase[1, :, lanes]
+                pieces.append(
+                    jnp.concatenate(
+                        [cos_o * boxes[g][o : o + 1, :] + sin_o * turned[g][o : o + 1, :] for g in range(size)], 0
+                    )
+                )
+            result = product(pieces)
+            for g in range(size):
+                three[first + start + g] = result[g * padded : (g + 1) * padded]
+
+    level_three(half * blks)
+    for step in range(blks):
+        each(halves, lambda e: forward(lax.rem(blk + step, blks), e).wait_recv())
+    for e in range(1, halves):
+        level_three(lax.rem(half + e, halves) * blks)
+
     for q in range(groups // OCT):
-        boxes = [low[q * OCT + g] for g in range(OCT)]
-        turned = [pltpu.roll(box, width // 2, 1) for box in boxes]
-        pieces = []
-        for o in range(OCT):
-            lanes = slice(o * width, (o + 1) * width)
-            cos_o, sin_o = phase[0, :, lanes], phase[1, :, lanes]
-            pieces.append(
-                jnp.concatenate(
-                    [cos_o * boxes[g][o : o + 1, :] + sin_o * turned[g][o : o + 1, :] for g in range(OCT)], 0
-                )
-            )
-        three = product(pieces)
         pieces = []
         for o in range(OCT):
             lanes = slice(o * width, (o + 1) * width)
             column = q * OCT + o
-            box = three[o * padded : (o + 1) * padded] * keep3[:, column : column + 1]
+            box = three[column] * keep3[:, column : column + 1]
             pieces.append(phase[2, :, lanes] * box + phase[3, :, lanes] * pltpu.roll(box, width // 2, 1))
         keep4 = jnp.sum(jnp.where(diagonal, need4[q : q + 1, :].astype(F32), 0.0), 1, keepdims=True)
         four = product(pieces) * keep4
         cone_out[:, q, :] = four[:cones]
+
+    each(blks * subs, lambda d: copy(d).wait_send())
+    for step in range(blks):
+        each(halves, lambda e: forward(lax.rem(blk + step, blks), e).wait_send())
 
 
 def put_out(low_ref, cone_ref, low_out, cone_out, sems):
@@ -302,6 +315,7 @@
                 pltpu.VMEM((pairs, width), F32),
                 pltpu.VMEM((blks, subs, per_sub, width), F32),
                 pltpu.VMEM((groups, per_sub, width), F32),
+                pltpu.VMEM((groups, padded, width), F32),
                 pltpu.VMEM((4, padded, OCT * width), F32),
                 pltpu.SemaphoreType.DMA((7,)),
                 pltpu.SemaphoreType.DMA((blks * subs,)),

time: 13.6 us -> 13.5 us (level)
  the two profiles are of different devices: /device:TPU:0 before, /device:TPU:1 now
where the time goes in v3:
time: 13.5 us; the launch traced here: 13.4 us
  Pallas kernels  12.7 us (94%)
  between operations  0.64 us (5%)
    pallas_call x1, Pallas kernels, local(): pl.pallas_call(functools.partial(kernel, halves, blks, subs, cones), out_...  12.1 us
    pallas_call x1, Pallas kernels, local(): pl.pallas_call(put_out, out_shape=[jax.ShapeDtypeStruct(value.shape, F32)...  0.61 us

profile of v3, /device:TPU:1, one launch (start us, length us, event | category | flops | bytes accessed | tf_op | source)
XLA Modules:
  0.0 13.4 jit_solution(3872851338590189838)
XLA Ops:
  0.6 12.1 %upward.1 = (f32[8,128]{1,0:T(8,128)S(1)}, f32[6,1,128]{2,1,0:T(1,128)S(1)}) custom-call(f32[512,128]{1,0:T(8,128)} %leaf_hbm.1, s32[4,128]{1,0:T(4,128)} %bitcast.2, f32[2,48]{1,0:T(2,128)} %angle_hbm.1, s32[6,8]{1,0:T(8,128)} %need3_hbm.1, s32[1,6]{1,0:T(1,128)} %bitcast.3, bf16[1024,256]{1,0:T(8,128)(2,1)} %constant.4.clone.weight_hbm, ...), custom_call_target="tpu_custom_call" | custom-call | tf_op jit(solution)/shard_map/upward/pallas_call | solution.py:299
  12.7 0.6 %put_out.1 = (f32[8,128]{1,0:T(8,128)}, f32[6,1,128]{2,1,0:T(1,128)}) custom-call(f32[8,128]{1,0:T(8,128)S(1)} %get-tuple-element.4.low_ref, f32[6,1,128]{2,1,0:T(1,128)S(1)} %get-tuple-element.5.cone_ref), custom_call_target="tpu_custom_call" | custom-call | tf_op jit(solution)/shard_map/put_out/pallas_call | solution.py:330
